TPU v7x, 32 devices: a whole 2x2x4 slice. The times are simulated.
32 devices in a mesh: prow: 8 (over y, x, core), pcol: 4 (over z).
Axes of the slice: x: 2, y: 2, z: 4, core: 2. Of those that a mesh axis runs over, the one named last changes fastest.
Arguments:
- rhs: bfloat16 [128, 64, 256], P('prow'), may hold values from -6 to 6
- blocks: bfloat16 [128, 16, 256, 256], P('prow', 'pcol'), may hold values from -0.0625 to 0.0625
- inverses: bfloat16 [128, 256, 256], P('prow'), may hold values from -1 to 2.1, as said below
- columns: int32 [128, 16], P('prow', 'pcol'), may hold values from 0 to 127, as said below
- counts: int32 [128, 4], P('prow', 'pcol'), may hold values from 0 to 4, as said below
Outputs:
- solved: bfloat16 [128, 64, 256], P('prow')
Inputs may be any that keep to these rules, and one draw needn't show every extreme that they name: `columns`: slot c of array row o names a block row k (level order) of an earlier level than that of o, with (k // 8) % 4 == c // 4, or 0 where no such block row exists; only the first counts[o, c // 4] slots of a group are used. `counts`: 0 where the group has no earlier block row (level 0 in particular); otherwise 1 or more. `inverses`: each tile is the inverse of a lower triangular diagonal block, itself lower triangular.
All inputs are finite; a program needn't handle non-finite values.
Results may differ from a plain program's by a relative error of at most 0.0054.
Values may be sent and summed in bfloat16 or wider, within the bound.
No kernel may reach another device: no remote copies, remote signals or barrier semaphores. Data moves between devices by JAX's collectives and lax.ppermute only.
A program may use at most 64 MiB of HBM per device.

v0:
```python
import jax
import jax.numpy as jnp
from jax import lax
from jax.sharding import PartitionSpec as P

LEVELS = 8
LR = 2


def body(rhs, blocks, inverses, columns, counts):
    side_count = rhs.shape[1]
    block_size = rhs.shape[2]
    prow_count = lax.axis_size("prow")
    pcol_count = lax.axis_size("pcol")
    per_level = LR * prow_count
    slot_count = columns.shape[1]
    active_mask = (jnp.arange(slot_count, dtype=jnp.int32)[None, :] < counts).astype(jnp.bfloat16)
    store_rows = LEVELS * prow_count
    solved_store = jnp.zeros((store_rows, side_count, block_size), jnp.bfloat16)
    solution = jnp.zeros(rhs.shape, jnp.bfloat16)

    def advance(level_no, carry):
        solved_store, solution = carry
        first_row = level_no * LR
        column_ids = lax.dynamic_slice_in_dim(columns, first_row, LR, 0)
        active = lax.dynamic_slice_in_dim(active_mask, first_row, LR, 0)
        panels = lax.dynamic_slice_in_dim(blocks, first_row, LR, 0)
        right_side = lax.dynamic_slice_in_dim(rhs, first_row, LR, 0)
        inverse_tiles = lax.dynamic_slice_in_dim(inverses, first_row, LR, 0)
        store_ids = column_ids // per_level * prow_count + column_ids % prow_count
        gathered = jnp.take(solved_store, store_ids, axis=0) * active[:, :, None, None]
        update_sum = jnp.einsum(
            "scrj,scij->sri", gathered, panels, preferred_element_type=jnp.float32
        )
        which_half = (lax.axis_index("pcol") - level_no * LR) % pcol_count
        keep_half = (which_half < LR).astype(jnp.bfloat16)
        half_index = jnp.minimum(which_half, LR - 1)
        summed = lax.psum(update_sum, "pcol")
        residual = (right_side.astype(jnp.float32) - summed).astype(jnp.bfloat16)
        solved_now = jnp.einsum(
            "srb,sab->sra", residual, inverse_tiles, preferred_element_type=jnp.float32
        ).astype(jnp.bfloat16)
        payload = lax.dynamic_index_in_dim(solved_now, half_index, 0, keepdims=True) * keep_half
        level_block = lax.all_gather(payload[None], "prow", axis=0, tiled=True)
        column_block = level_block.reshape((prow_count, side_count, block_size))
        solved_store = lax.dynamic_update_slice_in_dim(
            solved_store, column_block, level_no * prow_count, 0
        )
        solution = lax.dynamic_update_slice_in_dim(solution, solved_now, first_row, 0)
        return (solved_store, solution)

    solved_store, solution = lax.fori_loop(0, LEVELS, advance, (solved_store, solution))
    return solution


def solution(mesh):
    placed = (
        P("prow", None, None),
        P("prow", "pcol", None, None),
        P("prow", None, None),
        P("prow", "pcol"),
        P("prow", "pcol"),
    )
    return jax.shard_map(
        body, mesh=mesh, in_specs=placed, out_specs=P("prow", None, None), check_vma=False
    )
```

profile of v0, /device:TPU:0, one launch (start us, length us, event | category | flops | bytes accessed | tf_op | source)
XLA Modules:
  0.0 398.1 jit_solution(2024207592908420231)
XLA Ops:
  8.3 382.1 %while.18 = (s32[]{:T(128)}, bf16[64,64,256]{2,1,0:T(8,128)(2,1)S(1)}, bf16[16,64,256]{2,1,0:T(8,128)(2,1)S(1)}, bf16[16,64,256]{2,1,0:T(8,128)(2,1)}, s32[16,4]...) while((s32[]{:T(128)}, ...), condition=%wide.region_2.3_spmd, body=%wide.region_0.2_spmd.sunk | while | flops 84329728 | bytes 4233478 | solution.py:52
  9.1 2.3 convolution_bitcast_fusion.2
  11.5 37.5 %all-reduce.2.cloned.1.call-done = f32[2,64,256]{2,1,0:T(8,128)} async-done(((f32[2,64,256]{2,1,0:T(8,128)}), f32[2,64,256]{2,1,0:T(8,128)}) %all-reduce.2.cloned.1.call-update) | async-done | bytes 131088 | tf_op jit(solution)/shard_map/while/body/eval_jaxpr/psum | solution.py:38
  49.0 1.3 constant_dynamic-update-slice_fusion.4
  50.2 9.2 %all-gather.2 = bf16[8,64,256]{2,1,0:T(8,128)(2,1)S(1)} all-gather(bf16[1,64,256]{2,1,0:T(8,128)(2,1)S(1)} %dynamic-slice_multiply_fusion.2), channel_id=2, replica_groups=mesh['prow'=8,'pcol'=4] {'prow'}, dimensions={0}, use_global_device_ids=true | all-gather | bytes 294912 | tf_op jit(solution)/shard_map/while/body/eval_jaxpr/all_gather | solution.py:44
  60.3 2.3 convolution_bitcast_fusion.2
  62.7 33.6 %all-reduce.2.cloned.1.call-done = f32[2,64,256]{2,1,0:T(8,128)} async-done(((f32[2,64,256]{2,1,0:T(8,128)}), f32[2,64,256]{2,1,0:T(8,128)}) %all-reduce.2.cloned.1.call-update) | async-done | bytes 131088 | tf_op jit(solution)/shard_map/while/body/eval_jaxpr/psum | solution.py:38
  96.2 1.3 constant_dynamic-update-slice_fusion.4
  97.5 9.2 %all-gather.2 = bf16[8,64,256]{2,1,0:T(8,128)(2,1)S(1)} all-gather(bf16[1,64,256]{2,1,0:T(8,128)(2,1)S(1)} %dynamic-slice_multiply_fusion.2), channel_id=2, replica_groups=mesh['prow'=8,'pcol'=4] {'prow'}, dimensions={0}, use_global_device_ids=true | all-gather | bytes 294912 | tf_op jit(solution)/shard_map/while/body/eval_jaxpr/all_gather | solution.py:44
  107.6 2.3 convolution_bitcast_fusion.2
  110.0 33.5 %all-reduce.2.cloned.1.call-done = f32[2,64,256]{2,1,0:T(8,128)} async-done(((f32[2,64,256]{2,1,0:T(8,128)}), f32[2,64,256]{2,1,0:T(8,128)}) %all-reduce.2.cloned.1.call-update) | async-done | bytes 131088 | tf_op jit(solution)/shard_map/while/body/eval_jaxpr/psum | solution.py:38
  143.5 1.3 constant_dynamic-update-slice_fusion.4
  144.8 9.2 %all-gather.2 = bf16[8,64,256]{2,1,0:T(8,128)(2,1)S(1)} all-gather(bf16[1,64,256]{2,1,0:T(8,128)(2,1)S(1)} %dynamic-slice_multiply_fusion.2), channel_id=2, replica_groups=mesh['prow'=8,'pcol'=4] {'prow'}, dimensions={0}, use_global_device_ids=true | all-gather | bytes 294912 | tf_op jit(solution)/shard_map/while/body/eval_jaxpr/all_gather | solution.py:44
  154.8 2.3 convolution_bitcast_fusion.2
  157.2 33.5 %all-reduce.2.cloned.1.call-done = f32[2,64,256]{2,1,0:T(8,128)} async-done(((f32[2,64,256]{2,1,0:T(8,128)}), f32[2,64,256]{2,1,0:T(8,128)}) %all-reduce.2.cloned.1.call-update) | async-done | bytes 131088 | tf_op jit(solution)/shard_map/while/body/eval_jaxpr/psum | solution.py:38
  190.8 1.3 constant_dynamic-update-slice_fusion.4
  192.1 9.2 %all-gather.2 = bf16[8,64,256]{2,1,0:T(8,128)(2,1)S(1)} all-gather(bf16[1,64,256]{2,1,0:T(8,128)(2,1)S(1)} %dynamic-slice_multiply_fusion.2), channel_id=2, replica_groups=mesh['prow'=8,'pcol'=4] {'prow'}, dimensions={0}, use_global_device_ids=true | all-gather | bytes 294912 | tf_op jit(solution)/shard_map/while/body/eval_jaxpr/all_gather | solution.py:44
  202.1 2.3 convolution_bitcast_fusion.2
  204.5 33.5 %all-reduce.2.cloned.1.call-done = f32[2,64,256]{2,1,0:T(8,128)} async-done(((f32[2,64,256]{2,1,0:T(8,128)}), f32[2,64,256]{2,1,0:T(8,128)}) %all-reduce.2.cloned.1.call-update) | async-done | bytes 131088 | tf_op jit(solution)/shard_map/while/body/eval_jaxpr/psum | solution.py:38
  238.1 1.3 constant_dynamic-update-slice_fusion.4
  239.3 9.2 %all-gather.2 = bf16[8,64,256]{2,1,0:T(8,128)(2,1)S(1)} all-gather(bf16[1,64,256]{2,1,0:T(8,128)(2,1)S(1)} %dynamic-slice_multiply_fusion.2), channel_id=2, replica_groups=mesh['prow'=8,'pcol'=4] {'prow'}, dimensions={0}, use_global_device_ids=true | all-gather | bytes 294912 | tf_op jit(solution)/shard_map/while/body/eval_jaxpr/all_gather | solution.py:44
  249.4 2.3 convolution_bitcast_fusion.2
  251.8 33.5 %all-reduce.2.cloned.1.call-done = f32[2,64,256]{2,1,0:T(8,128)} async-done(((f32[2,64,256]{2,1,0:T(8,128)}), f32[2,64,256]{2,1,0:T(8,128)}) %all-reduce.2.cloned.1.call-update) | async-done | bytes 131088 | tf_op jit(solution)/shard_map/while/body/eval_jaxpr/psum | solution.py:38
  285.3 1.3 constant_dynamic-update-slice_fusion.4
  286.6 9.2 %all-gather.2 = bf16[8,64,256]{2,1,0:T(8,128)(2,1)S(1)} all-gather(bf16[1,64,256]{2,1,0:T(8,128)(2,1)S(1)} %dynamic-slice_multiply_fusion.2), channel_id=2, replica_groups=mesh['prow'=8,'pcol'=4] {'prow'}, dimensions={0}, use_global_device_ids=true | all-gather | bytes 294912 | tf_op jit(solution)/shard_map/while/body/eval_jaxpr/all_gather | solution.py:44
  296.7 2.3 convolution_bitcast_fusion.2
  299.1 33.5 %all-reduce.2.cloned.1.call-done = f32[2,64,256]{2,1,0:T(8,128)} async-done(((f32[2,64,256]{2,1,0:T(8,128)}), f32[2,64,256]{2,1,0:T(8,128)}) %all-reduce.2.cloned.1.call-update) | async-done | bytes 131088 | tf_op jit(solution)/shard_map/while/body/eval_jaxpr/psum | solution.py:38
  333.9 9.2 %all-gather.2 = bf16[8,64,256]{2,1,0:T(8,128)(2,1)S(1)} all-gather(bf16[1,64,256]{2,1,0:T(8,128)(2,1)S(1)} %dynamic-slice_multiply_fusion.2), channel_id=2, replica_groups=mesh['prow'=8,'pcol'=4] {'prow'}, dimensions={0}, use_global_device_ids=true | all-gather | bytes 294912 | tf_op jit(solution)/shard_map/while/body/eval_jaxpr/all_gather | solution.py:44
  343.9 2.3 convolution_bitcast_fusion.2
  346.4 33.5 %all-reduce.2.cloned.1.call-done = f32[2,64,256]{2,1,0:T(8,128)} async-done(((f32[2,64,256]{2,1,0:T(8,128)}), f32[2,64,256]{2,1,0:T(8,128)}) %all-reduce.2.cloned.1.call-update) | async-done | bytes 131088 | tf_op jit(solution)/shard_map/while/body/eval_jaxpr/psum | solution.py:38
  379.9 1.3 constant_dynamic-update-slice_fusion.4
  381.2 9.2 %all-gather.2 = bf16[8,64,256]{2,1,0:T(8,128)(2,1)S(1)} all-gather(bf16[1,64,256]{2,1,0:T(8,128)(2,1)S(1)} %dynamic-slice_multiply_fusion.2), channel_id=2, replica_groups=mesh['prow'=8,'pcol'=4] {'prow'}, dimensions={0}, use_global_device_ids=true | all-gather | bytes 294912 | tf_op jit(solution)/shard_map/while/body/eval_jaxpr/all_gather | solution.py:44
  (79 shorter events, 10.1 us)
Async XLA Ops:
  8.3 40.6 %all-reduce.2.cloned.1.call-start = ((), (), s32[]{:S(2)}) async-start(), calls=%async_computation | async-start | bytes 262144 | tf_op jit(solution)/shard_map/while/body/eval_jaxpr/psum | solution.py:38
  59.5 36.7 %all-reduce.2.cloned.1.call-start = ((), (), s32[]{:S(2)}) async-start(), calls=%async_computation | async-start | bytes 262144 | tf_op jit(solution)/shard_map/while/body/eval_jaxpr/psum | solution.py:38
  106.8 36.7 %all-reduce.2.cloned.1.call-start = ((), (), s32[]{:S(2)}) async-start(), calls=%async_computation | async-start | bytes 262144 | tf_op jit(solution)/shard_map/while/body/eval_jaxpr/psum | solution.py:38
  154.1 36.7 %all-reduce.2.cloned.1.call-start = ((), (), s32[]{:S(2)}) async-start(), calls=%async_computation | async-start | bytes 262144 | tf_op jit(solution)/shard_map/while/body/eval_jaxpr/psum | solution.py:38
  201.4 36.7 %all-reduce.2.cloned.1.call-start = ((), (), s32[]{:S(2)}) async-start(), calls=%async_computation | async-start | bytes 262144 | tf_op jit(solution)/shard_map/while/body/eval_jaxpr/psum | solution.py:38
  248.6 36.7 %all-reduce.2.cloned.1.call-start = ((), (), s32[]{:S(2)}) async-start(), calls=%async_computation | async-start | bytes 262144 | tf_op jit(solution)/shard_map/while/body/eval_jaxpr/psum | solution.py:38
  295.9 36.7 %all-reduce.2.cloned.1.call-start = ((), (), s32[]{:S(2)}) async-start(), calls=%async_computation | async-start | bytes 262144 | tf_op jit(solution)/shard_map/while/body/eval_jaxpr/psum | solution.py:38
  343.2 36.7 %all-reduce.2.cloned.1.call-start = ((), (), s32[]{:S(2)}) async-start(), calls=%async_computation | async-start | bytes 262144 | tf_op jit(solution)/shard_map/while/body/eval_jaxpr/psum | solution.py:38
  390.4 0.8 copy-start
Sparse Core Ops, SparseCore 0:
  11.6 37.3 all-reduce.1
  62.8 33.4 all-reduce.1
  110.1 33.4 all-reduce.1
  157.3 33.4 all-reduce.1
  204.6 33.4 all-reduce.1
  251.9 33.4 all-reduce.1
  299.2 33.4 all-reduce.1
  346.4 33.4 all-reduce.1
where the time goes:
time: 399 us; the launch traced here: 398 us
  waiting for transfers between devices  272 us (68%)
  blocking collectives  74 us (19%)
  matrix products  28.7 us (7%)
  between operations  13.4 us (3%)
  local copies, waits for them, and re-layouts  7.25 us (2%)
    psum x8, waiting for transfers between devices, advance(): summed = lax.psum(update_sum, 'pcol')  272 us
    all_gather x8, blocking collectives, advance(): level_block = lax.all_gather(payload[None], 'prow', axis=0, tiled=True)  74 us
    dot_general x8, matrix products, advance(): jnp.einsum('scrj,scij->sri', gathered, panels, preferred_element_type=jnp...  18.7 us
    dot_general x8, matrix products, advance(): jnp.einsum('srb,sab->sra', residual, inverse_tiles, preferred_element_typ...  10 us
  transfers between devices with their start and end apart: 8, of which 8 were waited for; matrix products, arithmetic and copies ran while one was open for 0% of the time, Pallas kernels for 0%

commit v1 on v0

--- a/solution.py
+++ b/solution.py
@@ -35,7 +35,7 @@
         which_half = (lax.axis_index("pcol") - level_no * LR) % pcol_count
         keep_half = (which_half < LR).astype(jnp.bfloat16)
         half_index = jnp.minimum(which_half, LR - 1)
-        summed = lax.psum(update_sum, "pcol")
+        summed = jnp.sum(lax.all_gather(update_sum, "pcol"), axis=0)
         residual = (right_side.astype(jnp.float32) - summed).astype(jnp.bfloat16)
         solved_now = jnp.einsum(
             "srb,sab->sra", residual, inverse_tiles, preferred_element_type=jnp.float32

time: 399 us -> 238 us (0.60)
  waiting for transfers between devices: 272 us -> 0 us
  blocking collectives: 74 us -> 205 us
  between operations: 13.4 us -> 0.03 us
  matrix products: 28.7 us -> 23 us
    psum x8 -> x0, waiting for transfers between devices: 272 us -> none  [advance(): summed = lax.psum(update_sum, 'pcol')]
    all_gather x0 -> x8, blocking collectives: none -> 134 us  [advance(): summed = jnp.sum(lax.all_gather(update_sum, 'pcol'), axis=0)]
    dot_general x8, matrix products: 18.7 us -> 13.4 us  [advance(): jnp.einsum('scrj,scij->sri', gathered, panels, preferred_element_type=jnp...]
  transfers between devices with their start and end apart: 8 -> 0, of which waited for: 8 -> 0; matrix products, arithmetic and copies ran while one was open for 0% -> 0% of each run, Pallas kernels for 0% -> 0%
where the time goes in v1:
time: 238 us
  blocking collectives  205 us (86%)
  matrix products  23 us (10%)
  local copies, waits for them, and re-layouts  7.25 us (3%)
    all_gather x8, blocking collectives, advance(): summed = jnp.sum(lax.all_gather(update_sum, 'pcol'), axis=0)  134 us
    all_gather x8, blocking collectives, advance(): level_block = lax.all_gather(payload[None], 'prow', axis=0, tiled=True)  71.4 us
    dot_general x8, matrix products, advance(): jnp.einsum('scrj,scij->sri', gathered, panels, preferred_element_type=jnp...  13.4 us
    dot_general x8, matrix products, advance(): jnp.einsum('srb,sab->sra', residual, inverse_tiles, preferred_element_typ...  9.58 us

profile of v1, /device:TPU:0, one launch (start us, length us, event | category | flops | bytes accessed | tf_op | source)
XLA Modules:
  0.0 237.6 jit_solution(15262697398195278164)
XLA Ops:
  1.8 235.0 %while.18 = (s32[]{:T(128)}, bf16[64,64,256]{2,1,0:T(8,128)(2,1)S(1)}, bf16[16,64,256]{2,1,0:T(8,128)(2,1)S(1)}, bf16[16,64,256]{2,1,0:T(8,128)(2,1)}, s32[16,4]...) while((s32[]{:T(128)}, ...), condition=%wide.region_2.3_spmd, body=%wide.region_0.2_spmd.sunk | while | flops 84395264 | bytes 4757738 | solution.py:52
  2.6 1.7 convolution_bitcast_fusion.2
  4.2 17.4 %all-gather.4 = f32[8,64,256]{2,1,0:T(8,128)S(1)} all-gather(f32[2,64,256]{2,1,0:T(8,128)S(1)} %convolution_bitcast_fusion.2), channel_id=2, replica_groups=mesh['prow'=8,'pcol'=4] {'pcol'}, dimensions={0}, use_global_device_ids=true | all-gather | bytes 655360 | tf_op jit(solution)/shard_map/while/body/eval_jaxpr/all_gather | solution.py:38
  21.6 1.2 constant_dynamic-update-slice_fusion.4
  22.9 9.3 %all-gather.5 = bf16[8,64,256]{2,1,0:T(8,128)(2,1)S(1)} all-gather(bf16[1,64,256]{2,1,0:T(8,128)(2,1)S(1)} %dynamic-slice_multiply_fusion.2), channel_id=3, replica_groups=mesh['prow'=8,'pcol'=4] {'prow'}, dimensions={0}, use_global_device_ids=true | all-gather | bytes 294912 | tf_op jit(solution)/shard_map/while/body/eval_jaxpr/all_gather | solution.py:44
  33.0 1.7 convolution_bitcast_fusion.2
  34.6 16.8 %all-gather.4 = f32[8,64,256]{2,1,0:T(8,128)S(1)} all-gather(f32[2,64,256]{2,1,0:T(8,128)S(1)} %convolution_bitcast_fusion.2), channel_id=2, replica_groups=mesh['prow'=8,'pcol'=4] {'pcol'}, dimensions={0}, use_global_device_ids=true | all-gather | bytes 655360 | tf_op jit(solution)/shard_map/while/body/eval_jaxpr/all_gather | solution.py:38
  51.5 1.2 constant_dynamic-update-slice_fusion.4
  52.7 9.3 %all-gather.5 = bf16[8,64,256]{2,1,0:T(8,128)(2,1)S(1)} all-gather(bf16[1,64,256]{2,1,0:T(8,128)(2,1)S(1)} %dynamic-slice_multiply_fusion.2), channel_id=3, replica_groups=mesh['prow'=8,'pcol'=4] {'prow'}, dimensions={0}, use_global_device_ids=true | all-gather | bytes 294912 | tf_op jit(solution)/shard_map/while/body/eval_jaxpr/all_gather | solution.py:44
  62.8 1.7 convolution_bitcast_fusion.2
  64.5 16.6 %all-gather.4 = f32[8,64,256]{2,1,0:T(8,128)S(1)} all-gather(f32[2,64,256]{2,1,0:T(8,128)S(1)} %convolution_bitcast_fusion.2), channel_id=2, replica_groups=mesh['prow'=8,'pcol'=4] {'pcol'}, dimensions={0}, use_global_device_ids=true | all-gather | bytes 655360 | tf_op jit(solution)/shard_map/while/body/eval_jaxpr/all_gather | solution.py:38
  81.1 1.2 constant_dynamic-update-slice_fusion.4
  82.3 8.3 %all-gather.5 = bf16[8,64,256]{2,1,0:T(8,128)(2,1)S(1)} all-gather(bf16[1,64,256]{2,1,0:T(8,128)(2,1)S(1)} %dynamic-slice_multiply_fusion.2), channel_id=3, replica_groups=mesh['prow'=8,'pcol'=4] {'prow'}, dimensions={0}, use_global_device_ids=true | all-gather | bytes 294912 | tf_op jit(solution)/shard_map/while/body/eval_jaxpr/all_gather | solution.py:44
  91.5 1.7 convolution_bitcast_fusion.2
  93.1 16.6 %all-gather.4 = f32[8,64,256]{2,1,0:T(8,128)S(1)} all-gather(f32[2,64,256]{2,1,0:T(8,128)S(1)} %convolution_bitcast_fusion.2), channel_id=2, replica_groups=mesh['prow'=8,'pcol'=4] {'pcol'}, dimensions={0}, use_global_device_ids=true | all-gather | bytes 655360 | tf_op jit(solution)/shard_map/while/body/eval_jaxpr/all_gather | solution.py:38
  109.8 1.2 constant_dynamic-update-slice_fusion.4
  111.0 9.3 %all-gather.5 = bf16[8,64,256]{2,1,0:T(8,128)(2,1)S(1)} all-gather(bf16[1,64,256]{2,1,0:T(8,128)(2,1)S(1)} %dynamic-slice_multiply_fusion.2), channel_id=3, replica_groups=mesh['prow'=8,'pcol'=4] {'prow'}, dimensions={0}, use_global_device_ids=true | all-gather | bytes 294912 | tf_op jit(solution)/shard_map/while/body/eval_jaxpr/all_gather | solution.py:44
  121.1 1.7 convolution_bitcast_fusion.2
  122.7 16.6 %all-gather.4 = f32[8,64,256]{2,1,0:T(8,128)S(1)} all-gather(f32[2,64,256]{2,1,0:T(8,128)S(1)} %convolution_bitcast_fusion.2), channel_id=2, replica_groups=mesh['prow'=8,'pcol'=4] {'pcol'}, dimensions={0}, use_global_device_ids=true | all-gather | bytes 655360 | tf_op jit(solution)/shard_map/while/body/eval_jaxpr/all_gather | solution.py:38
  139.4 1.2 constant_dynamic-update-slice_fusion.4
  140.6 8.3 %all-gather.5 = bf16[8,64,256]{2,1,0:T(8,128)(2,1)S(1)} all-gather(bf16[1,64,256]{2,1,0:T(8,128)(2,1)S(1)} %dynamic-slice_multiply_fusion.2), channel_id=3, replica_groups=mesh['prow'=8,'pcol'=4] {'prow'}, dimensions={0}, use_global_device_ids=true | all-gather | bytes 294912 | tf_op jit(solution)/shard_map/while/body/eval_jaxpr/all_gather | solution.py:44
  149.7 1.7 convolution_bitcast_fusion.2
  151.4 16.6 %all-gather.4 = f32[8,64,256]{2,1,0:T(8,128)S(1)} all-gather(f32[2,64,256]{2,1,0:T(8,128)S(1)} %convolution_bitcast_fusion.2), channel_id=2, replica_groups=mesh['prow'=8,'pcol'=4] {'pcol'}, dimensions={0}, use_global_device_ids=true | all-gather | bytes 655360 | tf_op jit(solution)/shard_map/while/body/eval_jaxpr/all_gather | solution.py:38
  168.0 1.2 constant_dynamic-update-slice_fusion.4
  169.2 9.3 %all-gather.5 = bf16[8,64,256]{2,1,0:T(8,128)(2,1)S(1)} all-gather(bf16[1,64,256]{2,1,0:T(8,128)(2,1)S(1)} %dynamic-slice_multiply_fusion.2), channel_id=3, replica_groups=mesh['prow'=8,'pcol'=4] {'prow'}, dimensions={0}, use_global_device_ids=true | all-gather | bytes 294912 | tf_op jit(solution)/shard_map/while/body/eval_jaxpr/all_gather | solution.py:44
  179.3 1.7 convolution_bitcast_fusion.2
  181.0 16.6 %all-gather.4 = f32[8,64,256]{2,1,0:T(8,128)S(1)} all-gather(f32[2,64,256]{2,1,0:T(8,128)S(1)} %convolution_bitcast_fusion.2), channel_id=2, replica_groups=mesh['prow'=8,'pcol'=4] {'pcol'}, dimensions={0}, use_global_device_ids=true | all-gather | bytes 655360 | tf_op jit(solution)/shard_map/while/body/eval_jaxpr/all_gather | solution.py:38
  198.8 8.3 %all-gather.5 = bf16[8,64,256]{2,1,0:T(8,128)(2,1)S(1)} all-gather(bf16[1,64,256]{2,1,0:T(8,128)(2,1)S(1)} %dynamic-slice_multiply_fusion.2), channel_id=3, replica_groups=mesh['prow'=8,'pcol'=4] {'prow'}, dimensions={0}, use_global_device_ids=true | all-gather | bytes 294912 | tf_op jit(solution)/shard_map/while/body/eval_jaxpr/all_gather | solution.py:44
  207.9 1.7 convolution_bitcast_fusion.2
  209.6 16.6 %all-gather.4 = f32[8,64,256]{2,1,0:T(8,128)S(1)} all-gather(f32[2,64,256]{2,1,0:T(8,128)S(1)} %convolution_bitcast_fusion.2), channel_id=2, replica_groups=mesh['prow'=8,'pcol'=4] {'pcol'}, dimensions={0}, use_global_device_ids=true | all-gather | bytes 655360 | tf_op jit(solution)/shard_map/while/body/eval_jaxpr/all_gather | solution.py:38
  226.3 1.2 constant_dynamic-update-slice_fusion.4
  227.5 9.3 %all-gather.5 = bf16[8,64,256]{2,1,0:T(8,128)(2,1)S(1)} all-gather(bf16[1,64,256]{2,1,0:T(8,128)(2,1)S(1)} %dynamic-slice_multiply_fusion.2), channel_id=3, replica_groups=mesh['prow'=8,'pcol'=4] {'prow'}, dimensions={0}, use_global_device_ids=true | all-gather | bytes 294912 | tf_op jit(solution)/shard_map/while/body/eval_jaxpr/all_gather | solution.py:44
  (71 shorter events, 9.8 us)
Async XLA Ops:
  236.8 0.8 copy-start
